TPU v7x, 32 devices: a whole 2x2x4 slice. The times are simulated.
32 devices in a mesh: dp: 4 (over y, x), expert: 8 (over z, core).
Axes of the slice: x: 2, y: 2, z: 4, core: 2. Of those that a mesh axis runs over, the one named last changes fastest.
Arguments:
- tokens: bfloat16 [4096, 4096], P(('dp', 'expert')), may hold values from -6 to 6
- gate_proj: bfloat16 [8, 768, 4096], P('expert', 'dp'), may hold values from -0.09375 to 0.09375
- up_proj: bfloat16 [8, 768, 4096], P('expert', 'dp'), may hold values from -0.09375 to 0.09375
- down_proj: bfloat16 [8, 768, 4096], P('expert', 'dp'), may hold values from -0.21875 to 0.21875
- route_ids: int32 [4096, 2], P(('dp', 'expert')), may hold values from 0 to 7, as said below
- route_slots: int32 [4096, 2], P(('dp', 'expert')), may hold values from 0 to 95, as said below
- route_gates: float32 [4096, 2], P(('dp', 'expert')), may hold values from 0.1 to 1
- image_shard: int32 [4, 8], P(None, 'expert'), may hold values from 0 to 3, as said below
- norm_gain: float32 [4096], replicated, may hold values from 0.5 to 1.5
- key_proj: bfloat16 [4096, 1024], P('dp'), may hold values from -0.09375 to 0.09375
Outputs:
- student_rows: bfloat16 [4096, 4096], P(('dp', 'expert'))
- keys: bfloat16 [4096, 1024], P(('dp', 'expert'))
Inputs may be any that keep to these rules, and one draw needn't show every extreme that they name: `route_ids`: within the rows of one device a token names 2 different experts and no expert is named more than 2 * 48 times; on every device some expert is named exactly 2 * 48 times. `route_slots`: within the rows of one device the mentions of one expert carry the numbers 0 up to their count minus one, each once; one expert has 48 retained mentions from every device. `image_shard`: for each e, of the 4 image tiles of column e exactly 1 name each shard.
All inputs are finite; a program needn't handle non-finite values.
Results may differ from a plain program's by a relative error of at most 0.007.
Values may be sent and summed in bfloat16 or wider, within the bound.
A program may use at most 128 MiB of HBM per device.

v0:
```python
import jax
import jax.numpy as jnp
from jax import lax
from jax.sharding import PartitionSpec as P

IMG_TOK = 128


def normalize(values, norm_gain):
    wide = values.astype(jnp.float32)
    mean_square = jnp.mean(wide * wide, axis=-1, keepdims=True)
    return (wide * lax.rsqrt(mean_square + 1e-05) * norm_gain).astype(jnp.bfloat16)


def activate(incoming, gate_rows, up_rows):
    dims = (((1,), (1,)), ((), ()))
    gate_act = lax.dot_general(incoming, gate_rows, dims, preferred_element_type=jnp.float32)
    up_act = lax.dot_general(incoming, up_rows, dims, preferred_element_type=jnp.float32)
    return (jax.nn.silu(gate_act) * up_act).astype(jnp.bfloat16)


def per_device(
    tokens,
    gate_proj,
    up_proj,
    down_proj,
    route_ids,
    route_slots,
    route_gates,
    image_shard,
    norm_gain,
    key_proj,
):
    tok_dev, model_width = tokens.shape
    top_count = route_ids.shape[1]
    experts = gate_proj.shape[0] * lax.axis_size("expert")
    capacity = 3 * tok_dev * top_count // (2 * experts)
    slot_total = experts * capacity
    retained = route_slots < capacity
    slot_cells = jnp.where(retained, route_ids * capacity + route_slots, slot_total).reshape(-1)
    owners = jnp.arange(tok_dev * top_count, dtype=jnp.int32) // top_count
    cell_token = (
        jnp.full((slot_total + 1,), tok_dev, jnp.int32).at[slot_cells].set(owners)[:slot_total]
    )
    outgoing = jnp.take(tokens, cell_token, axis=0, mode="fill", fill_value=0).reshape(
        experts, capacity, model_width
    )
    arrived = lax.all_to_all(outgoing, "expert", split_axis=0, concat_axis=0, tiled=True)
    incoming = arrived.reshape(-1, model_width)
    hidden = activate(
        incoming,
        lax.all_gather(gate_proj, "dp", axis=1, tiled=True)[0],
        lax.all_gather(up_proj, "dp", axis=1, tiled=True)[0],
    )
    summed = jnp.dot(
        hidden,
        lax.all_gather(down_proj, "dp", axis=1, tiled=True)[0],
        preferred_element_type=jnp.float32,
    )
    produced = summed.astype(jnp.bfloat16).reshape(arrived.shape)
    returned = lax.all_to_all(produced, "expert", split_axis=0, concat_axis=0, tiled=True).reshape(
        -1, model_width
    )
    picked = jnp.take(returned, slot_cells, axis=0, mode="fill", fill_value=0).reshape(
        tok_dev, top_count, model_width
    )
    mixing = jnp.where(retained, route_gates, 0.0)
    branch = jnp.einsum("tk,tkd->td", mixing, picked.astype(jnp.float32))
    teacher = (tokens.astype(jnp.float32) + branch).astype(jnp.bfloat16)
    gathered = lax.all_gather(teacher, "dp", axis=0, tiled=True)
    shard_column = image_shard.reshape(-1)
    images_col = shard_column.shape[0]
    arrangement = jnp.argsort(shard_column * images_col + jnp.arange(images_col, dtype=jnp.int32))
    images = gathered.reshape(images_col, IMG_TOK, model_width)
    position = lax.axis_index("dp")
    ordered = jnp.take(images, arrangement, axis=0).reshape(images_col * IMG_TOK, model_width)
    student_rows = lax.dynamic_slice_in_dim(ordered, position * tok_dev, tok_dev, 0)
    normed = normalize(ordered, norm_gain)
    columns = lax.dynamic_slice_in_dim(normed, position * key_proj.shape[0], key_proj.shape[0], 1)
    projected = lax.psum_scatter(
        jnp.dot(columns, key_proj, preferred_element_type=jnp.float32),
        "dp",
        scatter_dimension=0,
        tiled=True,
    )
    return (student_rows, projected.astype(jnp.bfloat16))


def solution(mesh):
    in_specs = (
        P(("dp", "expert"), None),
        P("expert", "dp", None),
        P("expert", "dp", None),
        P("expert", "dp", None),
        P(("dp", "expert"), None),
        P(("dp", "expert"), None),
        P(("dp", "expert"), None),
        P(None, "expert"),
        P(),
        P("dp", None),
    )
    out_specs = (P(("dp", "expert"), None), P(("dp", "expert"), None))
    return jax.shard_map(
        per_device, mesh=mesh, in_specs=in_specs, out_specs=out_specs, check_vma=False
    )
```

profile of v0, /device:TPU:0, one launch (start us, length us, event | category | flops | bytes accessed | tf_op | source)
XLA Modules:
  0.0 443.4 jit_solution(14120629486726420632)
XLA Ops:
  7.2 0.0 copy-start
  7.2 0.0 copy-start.5
  7.2 0.0 copy-start.4
  7.2 0.0 copy-start.1
  7.2 0.0 all-gather.5.cloned.1.call-start
  7.3 0.7 all-gather.5.cloned.1.call-update
  7.9 0.0 all-gather.7.cloned.1.call-start
  8.0 0.7 all-gather.7.cloned.1.call-update
  8.7 0.0 all-gather.9.cloned.1.call-start
  8.7 0.7 all-gather.9.cloned.1.call-update
  9.4 0.0 copy-done.5
  9.4 0.0 copy-done.4
  9.5 0.1 copy.14
  9.6 0.1 reshape.128
  9.7 1.4 scatter_custom_fusion
  11.2 0.1 slice.6
  11.3 0.0 copy-done.1
  11.3 4.0 gather_fusion
  15.3 2.2 broadcast_select_fusion.1
  17.5 77.8 %all_to_all.10 = bf16[8,48,4096]{2,1,0:T(8,128)(2,1)} all-to-all(bf16[8,48,4096]{2,1,0:T(8,128)(2,1)S(1)} %broadcast_select_fusion.1), channel_id=1, replica_groups=mesh['dp'=4,'expert'=8] {'expert'}, dimensions={0} | all-to-all | bytes 6291456 | tf_op jit(solution)/shard_map/all_to_all | solution.py:48
  95.2 0.0 all-gather.5.cloned.1.call-done
  95.2 7.4 %fusion.4 = f32[384,768]{1,0:T(8,128)} fusion(bf16[384,4096]{1,0:T(8,128)(2,1)} %bitcast.45, bf16[1,768,4096]{2,1,0:T(8,128)(2,1)} %all-gather.5.cloned.1.call-done), kind=kOutput, calls=%fused_computation.9 | convolution fusion | flops 2415919104 | bytes 10616832 | tf_op jit(solution)/shard_map/dot_general | solution.py:17
  102.7 51.9 %all-gather.7.cloned.1.call-done = bf16[1,768,4096]{2,1,0:T(8,128)(2,1)} async-done(((bf16[1,192,4096]{2,1,0:T(8,128)(2,1)}), bf16[1,768,4096]{2,1,0:T(8,128)(2,1)}) %all-gather.7.cloned.1.call-update) | async-done | bytes 6291472 | tf_op jit(solution)/shard_map/all_gather | solution.py:53
  154.6 71.9 %all-gather.9.cloned.1.call-done = bf16[1,768,4096]{2,1,0:T(8,128)(2,1)} async-done(((bf16[1,192,4096]{2,1,0:T(8,128)(2,1)}), bf16[1,768,4096]{2,1,0:T(8,128)(2,1)}) %all-gather.9.cloned.1.call-update) | async-done | bytes 6291472 | tf_op jit(solution)/shard_map/all_gather | solution.py:57
  226.5 14.2 %fusion.6 = bf16[384,4096]{1,0:T(8,128)(2,1)} fusion(bf16[1,768,4096]{2,1,0:T(8,128)(2,1)} %all-gather.9.cloned.1.call-done, bf16[384,4096]{1,0:T(8,128)(2,1)} %bitcast.46, bf16[1,768,4096]{2,1,0:T(8,128)(2,1)} %all-gather.7.cloned.1.call-done, f32[384,768]{1,0:T(8,128)} %fusion.4), kind=kOutput, calls=%fused_computation.11 | convolution fusion | flops 4835180544 | bytes 20054016 | tf_op jit(solution)/shard_map/dot_general | solution.py:55
  240.6 0.0 copy-start.6
  240.7 4.7 %all-to-all-start.1 = ((bf16[8,48,4096]{2,1,0:T(8,128)(2,1)}), bf16[8,48,4096]{2,1,0:T(8,128)(2,1)}, u32[]{:S(2)}, u32[]{:S(2)}) async-start(bf16[8,48,4096]{2,1,0:T(8,128)(2,1)} %bitcast.44), calls=%async_computation.1 | async-start | bytes 6291456 | tf_op jit(solution)/shard_map/all_to_all | solution.py:61
  245.4 0.2 all-gather.11.cloned.1.call-start
  245.6 0.1 copy.13
  245.8 0.0 copy-done.6
  245.8 0.1 copy.15
  245.9 71.1 %all-to-all-done.1 = bf16[8,48,4096]{2,1,0:T(8,128)(2,1)} async-done(((bf16[8,48,4096]{2,1,0:T(8,128)(2,1)}), bf16[8,48,4096]{2,1,0:T(8,128)(2,1)}, u32[]{:S(2)}, u32[]{:S(2)}) %all-to-all-start.1) | async-done | bytes 3145760 | tf_op jit(solution)/shard_map/all_to_all | solution.py:61
  317.0 7.5 %gather_fusion.1 = bf16[256,4096]{1,0:T(8,128)(2,1)} fusion(bf16[384,4096]{1,0:T(8,128)(2,1)} %bitcast.10, s32[1024]{0:T(1024)S(1)} %pad_clamp_fusion.1), kind=kCustom, calls=%fused_computation.1 | custom fusion | bytes 4195328 | tf_op jit(solution)/shard_map/jit(_take)/gather | solution.py:64
  324.5 4.4 gather.21
  328.9 4.0 fusion.10
  332.9 0.0 copy-start.7
  332.9 2.2 fusion.9
  335.2 0.0 all-gather.11.cloned.1.call-update
  335.2 0.0 reduce-scatter.2.cloned.1.call-start
  335.3 0.0 copy-done.7
  335.3 0.7 sort.17
  336.1 0.1 broadcast_bitcast_fusion
  336.1 49.7 %all-gather.11.cloned.1.call-done = bf16[512,4096]{1,0:T(8,128)(2,1)} async-done(((bf16[128,4096]{1,0:T(8,128)(2,1)}), bf16[512,4096]{1,0:T(8,128)(2,1)}) %all-gather.11.cloned.1.call-update) | async-done | bytes 4194320 | tf_op jit(solution)/shard_map/all_gather | solution.py:70
  385.9 5.0 %gather_fusion.2 = bf16[4,128,4096]{2,1,0:T(8,128)(2,1)} fusion(bf16[4,128,4096]{2,1,0:T(8,128)(2,1)} %bitcast.43, s32[1024]{0:T(1024)S(1)} %pad_clamp_fusion), kind=kCustom, calls=%fused_computation.2 | custom fusion | bytes 8388624 | tf_op jit(solution)/shard_map/jit(_take)/gather | solution.py:76
  390.9 0.0 copy-start.2
  390.9 3.6 multiply_reduce_fusion
  394.4 0.0 copy-done.2
  394.4 0.0 dynamic-slice-start
  394.4 0.7 bitcast_select_fusion
  395.2 0.0 copy-start.3
  395.2 1.9 copy-done.3
  397.1 0.0 copy-done
  397.1 0.0 dynamic-slice-done
  397.1 2.6 fusion.17
  399.8 0.0 reduce-scatter.2.cloned.1.call-update
  399.8 2.3 constant_dynamic-slice_fusion
  402.1 33.0 %reduce-scatter.2.cloned.1.call-done = f32[128,1024]{1,0:T(8,128)} async-done(((f32[512,1024]{1,0:T(8,128)}), f32[128,1024]{1,0:T(8,128)}) %reduce-scatter.2.cloned.1.call-update) | async-done | bytes 524304 | tf_op jit(solution)/shard_map/reduce_scatter | solution.py:80
  435.1 1.8 convert_element_type.32
  (14 shorter events, 0.1 us)
Async XLA Ops:
  7.2 390.0 %copy-start = (bf16[1024,1024]{1,0:T(8,128)(2,1)S(1)}, bf16[1024,1024]{1,0:T(8,128)(2,1)}, u32[]{:S(2)}) copy-start(bf16[1024,1024]{1,0:T(8,128)(2,1)} %param.19) | copy-start | bytes 6291460
  7.2 2.3 copy-start.5
  7.2 2.3 copy-start.4
  7.2 4.1 copy-start.1
  7.2 88.0 %all-gather.5.cloned.1.call-start = ((), (), s32[]{:S(2)}) async-start(), calls=%async_computation.3 | async-start | bytes 7864320 | tf_op jit(solution)/shard_map/all_gather | solution.py:52
  7.9 146.6 %all-gather.7.cloned.1.call-start = ((), (), s32[]{:S(2)}) async-start(), calls=%async_computation.4 | async-start | bytes 7864320 | tf_op jit(solution)/shard_map/all_gather | solution.py:53
  8.7 217.8 %all-gather.9.cloned.1.call-start = ((), (), s32[]{:S(2)}) async-start(), calls=%async_computation.5 | async-start | bytes 7864320 | tf_op jit(solution)/shard_map/all_gather | solution.py:57
  240.6 5.1 %copy-start.6 = (f32[128,2]{0,1:T(2,128)S(1)}, f32[128,2]{0,1:T(2,128)}, u32[]{:S(2)}) copy-start(f32[128,2]{0,1:T(2,128)} %param.16) | copy-start | bytes 3076
  240.7 76.3 %all-to-all-start.1 = ((bf16[8,48,4096]{2,1,0:T(8,128)(2,1)}), bf16[8,48,4096]{2,1,0:T(8,128)(2,1)}, u32[]{:S(2)}, u32[]{:S(2)}) async-start(bf16[8,48,4096]{2,1,0:T(8,128)(2,1)} %bitcast.44), calls=%async_computation.1 | async-start | bytes 6291456 | tf_op jit(solution)/shard_map/all_to_all | solution.py:61
  245.4 140.5 %all-gather.11.cloned.1.call-start = ((), (), s32[]{:S(2)}) async-start(), calls=%async_computation.6 | async-start | bytes 5242880 | tf_op jit(solution)/shard_map/all_gather | solution.py:70
  332.9 2.3 copy-start.7
  335.2 99.9 %reduce-scatter.2.cloned.1.call-start = ((), (), s32[]{:S(2)}) async-start(), calls=%async_computation.7 | async-start | bytes 2621440 | tf_op jit(solution)/shard_map/reduce_scatter | solution.py:80
  390.9 3.6 copy-start.2
  394.4 2.7 dynamic-slice-start
  395.2 1.9 copy-start.3
Sparse Core Ops, SparseCore 0:
  9.9 72.7 all-gather.4
  84.5 70.0 all-gather.6
  156.4 70.0 all-gather.8
  335.3 50.5 all-gather.10
  399.9 35.1 reduce-scatter.1
where the time goes:
time: 444 us; the launch traced here: 443 us
  waiting for transfers between devices  280 us (63%)
  blocking collectives  77.8 us (18%)
  matrix products  28.3 us (6%)
  local copies, waits for them, and re-layouts  27.3 us (6%)
  between operations  14 us (3%)
  other arithmetic  11.3 us (3%)
  starting transfers between devices  5.11 us (1%)
    all_to_all x1, blocking collectives, per_device(): lax.all_to_all(outgoing, 'expert', split_axis=0, concat_axis=0, tiled=True)  77.8 us
    all_gather x1, waiting for transfers between devices, per_device(): lax.all_gather(down_proj, 'dp', axis=1, tiled=True)[0]  71.9 us
    all_to_all x1, waiting for transfers between devices, per_device(): lax.all_to_all(produced, 'expert', split_axis=0, concat_axis=0, tiled=True)  71.1 us
    all_gather x1, waiting for transfers between devices, per_device(): lax.all_gather(up_proj, 'dp', axis=1, tiled=True)[0]  51.9 us
    all_gather x1, waiting for transfers between devices, per_device(): gathered = lax.all_gather(teacher, 'dp', axis=0, tiled=True)  49.7 us
    reduce_scatter x1, waiting for transfers between devices, per_device(): lax.psum_scatter(jnp.dot(columns, key_proj, preferred_element_type=jnp.fl...  33 us
    dot_general x1, matrix products, per_device(): jnp.dot(hidden, lax.all_gather(down_proj, 'dp', axis=1, tiled=True)[0], p...  14.2 us
    gather x2, local copies, waits for them, and re-layouts, per_device(): jnp.take(returned, slot_cells, axis=0, mode='fill', fill_value=0)  11.9 us
  transfers between devices with their start and end apart: 6, of which 5 were waited for; matrix products, arithmetic and copies ran while one was open for 4% of the time, Pallas kernels for 0%

commit v1 on v0

--- a/solution.py
+++ b/solution.py
@@ -1,6 +1,10 @@
+import functools
+
 import jax
 import jax.numpy as jnp
 from jax import lax
+from jax.experimental import pallas as pl
+from jax.experimental.pallas import tpu as pltpu
 from jax.sharding import PartitionSpec as P
 
 IMG_TOK = 128
@@ -17,6 +21,395 @@
     gate_act = lax.dot_general(incoming, gate_rows, dims, preferred_element_type=jnp.float32)
     up_act = lax.dot_general(incoming, up_rows, dims, preferred_element_type=jnp.float32)
     return (jax.nn.silu(gate_act) * up_act).astype(jnp.bfloat16)
+
+
+CHUNKS = 4
+MESH = pl.DeviceIdType.MESH
+
+
+def fused_kernel(
+    n_expert,
+    capacity,
+    spread_ref,
+    mix_ref,
+    pick_ref,
+    gain_ref,
+    tokens_ref,
+    gate_ref,
+    up_ref,
+    down_ref,
+    key_ref,
+    student_ref,
+    keys_ref,
+    gate_buf,
+    up_buf,
+    down_buf,
+    key_buf,
+    outgoing,
+    incoming,
+    produced,
+    returned,
+    tiles,
+    hidden,
+    normed,
+    acc_gate,
+    acc_up,
+    send_sem,
+    recv_sem,
+    local_sem,
+):
+    d = lax.axis_index("dp")
+    e = lax.axis_index("expert")
+    dx = d + 1 - 2 * (d % 2)
+    dy = (d + 2) % 4
+    dd = (dx + 2) % 4
+    core = e % 2
+    sibling = e + 1 - 2 * core
+    tok_dev, width = tokens_ref.shape
+    units = gate_ref.shape[1]
+    half_units = units // 2
+    chunk = width // CHUNKS
+    key_rows, key_width = key_ref.shape
+    key_half = key_rows // 2
+    key_quarter = key_rows // 4
+    counts = {"remote": 0, "local": 0}
+
+    def send(source, target, where):
+        index = counts["remote"]
+        counts["remote"] += 1
+        copy = pltpu.make_async_remote_copy(
+            src_ref=source,
+            dst_ref=target,
+            send_sem=send_sem.at[index],
+            recv_sem=recv_sem.at[index],
+            device_id=where,
+            device_id_type=MESH,
+        )
+        copy.start()
+        return copy
+
+    def local(source, target):
+        index = counts["local"]
+        counts["local"] += 1
+        copy = pltpu.make_async_copy(source, target, local_sem.at[index])
+        copy.start()
+        return copy
+
+    to_x, to_y, to_sibling = {"dp": dx}, {"dp": dy}, {"expert": sibling}
+    peers = [lax.rem(e + k, n_expert) for k in range(1, n_expert)]
+    barrier = pltpu.get_barrier_semaphore()
+    for where in [to_x, to_y] + [{"expert": peer} for peer in peers]:
+        pl.semaphore_signal(barrier, inc=1, device_id=where, device_id_type=MESH)
+    pl.semaphore_wait(barrier, n_expert + 1)
+    sent = []
+
+    def tracked(*args):
+        copy = send(*args)
+        sent.append(copy)
+        return copy
+
+    gate_x = tracked(gate_ref.at[0], gate_buf.at[1], to_x)
+    gate_y = tracked(gate_ref.at[0], gate_buf.at[2], to_y)
+    up_x = tracked(up_ref.at[0], up_buf.at[1], to_x)
+    up_y = tracked(up_ref.at[0], up_buf.at[2], to_y)
+    own_gate = local(gate_ref.at[0], gate_buf.at[0])
+    own_up = local(up_ref.at[0], up_buf.at[0])
+    own_down = local(down_ref.at[0], down_buf.at[0])
+    own_key = local(key_ref, key_buf.at[0])
+
+    step = 512
+    spread = spread_ref[...]
+
+    def fill(i, carry):
+        cols = pl.ds(pl.multiple_of(i * step, step), step)
+        rows = jnp.dot(spread, tokens_ref[:, cols], preferred_element_type=jnp.float32)
+        outgoing[:, cols] = rows.astype(jnp.bfloat16)
+        return carry
+
+    lax.fori_loop(0, width // step, fill, 0)
+
+    def rows_of(owner):
+        return pl.ds(pl.multiple_of(owner * capacity, capacity), capacity)
+
+    mine = rows_of(e)
+    dispatched = [
+        tracked(outgoing.at[rows_of(peer), :], incoming.at[mine, :], {"expert": peer})
+        for peer in peers
+    ]
+    kept = local(outgoing.at[mine, :], incoming.at[mine, :])
+
+    low, high = pl.ds(0, half_units), pl.ds(half_units, half_units)
+    gate_y.wait_recv()
+    gate_d0 = tracked(gate_buf.at[2, low, :], gate_buf.at[3, low, :], to_x)
+    gate_x.wait_recv()
+    gate_d1 = tracked(gate_buf.at[1, high, :], gate_buf.at[3, high, :], to_y)
+    up_y.wait_recv()
+    up_d0 = tracked(up_buf.at[2, low, :], up_buf.at[3, low, :], to_x)
+    up_x.wait_recv()
+    up_d1 = tracked(up_buf.at[1, high, :], up_buf.at[3, high, :], to_y)
+
+    def down_own(c):
+        cols = pl.ds(c * chunk, chunk)
+        return (
+            tracked(down_ref.at[0, :, cols], down_buf.at[1, :, cols], to_x),
+            tracked(down_ref.at[0, :, cols], down_buf.at[2, :, cols], to_y),
+        )
+
+    downs = [down_own(0), down_own(1)]
+
+    for copy in dispatched:
+        copy.wait_recv()
+    kept.wait()
+    own_gate.wait()
+    own_up.wait()
+    dims = (((1,), (1,)), ((), ()))
+
+    def activate_slot(slot):
+        acc_gate[...] = jnp.zeros_like(acc_gate)
+        acc_up[...] = jnp.zeros_like(acc_up)
+
+        def add(i, carry):
+            cols = pl.ds(pl.multiple_of(i * step, step), step)
+            rows = incoming[:, cols]
+            acc_gate[...] += lax.dot_general(
+                rows, gate_buf[slot, :, cols], dims, preferred_element_type=jnp.float32
+            )
+            acc_up[...] += lax.dot_general(
+                rows, up_buf[slot, :, cols], dims, preferred_element_type=jnp.float32
+            )
+            return carry
+
+        lax.fori_loop(0, width // step, add, 0)
+        gate_act = acc_gate[...]
+        hidden[slot] = (gate_act / (1.0 + jnp.exp(-gate_act)) * acc_up[...]).astype(jnp.bfloat16)
+
+    def activate_loop(slot, carry):
+        activate_slot(slot)
+        return carry
+
+    lax.fori_loop(0, 3, activate_loop, 0)
+    for copy in (gate_d0, gate_d1, up_d0, up_d1):
+        copy.wait_recv()
+    activate_slot(3)
+    own_down.wait()
+
+    narrow = 256
+    hands = []
+    key_copies = []
+    my_half = pl.ds(pl.multiple_of(core * key_half, key_half), key_half)
+    quarter0 = pl.ds(pl.multiple_of(core * key_half, key_quarter), key_quarter)
+    quarter1 = pl.ds(pl.multiple_of(core * key_half + key_quarter, key_quarter), key_quarter)
+    for c in range(CHUNKS):
+        cols = pl.ds(c * chunk, chunk)
+        down_x, down_y = downs[c]
+        down_y.wait_recv()
+        d0 = tracked(down_buf.at[2, low, cols], down_buf.at[3, low, cols], to_x)
+        down_x.wait_recv()
+        d1 = tracked(down_buf.at[1, high, cols], down_buf.at[3, high, cols], to_y)
+        if c + 2 < CHUNKS:
+            downs.append(down_own(c + 2))
+        elif c + 1 == CHUNKS:
+            key_copies.append(tracked(key_ref.at[my_half, :], key_buf.at[1, my_half, :], to_x))
+            key_copies.append(tracked(key_ref.at[my_half, :], key_buf.at[2, my_half, :], to_y))
+        d0.wait_recv()
+        d1.wait_recv()
+
+        def project(i, carry):
+            at = pl.ds(pl.multiple_of(c * chunk + i * narrow, narrow), narrow)
+            total = jnp.dot(hidden[0], down_buf[0, :, at], preferred_element_type=jnp.float32)
+            for slot in range(1, 4):
+                total += jnp.dot(
+                    hidden[slot], down_buf[slot, :, at], preferred_element_type=jnp.float32
+                )
+            produced[:, at] = total.astype(jnp.bfloat16)
+            return carry
+
+        lax.fori_loop(0, chunk // narrow, project, 0)
+        back = [
+            tracked(produced.at[rows_of(peer), cols], returned.at[mine, cols], {"expert": peer})
+            for peer in peers
+        ]
+        hands.append((back, local(produced.at[mine, cols], returned.at[mine, cols])))
+
+    mix = mix_ref[...]
+    mix_hi = mix.astype(jnp.bfloat16)
+    mix_lo = (mix - mix_hi.astype(jnp.float32)).astype(jnp.bfloat16)
+    half_tok = tok_dev // 2
+    top, bottom = pl.ds(0, half_tok), pl.ds(half_tok, half_tok)
+    tile_sends = []
+    tile_diag = []
+
+    def combine(c):
+        back, own = hands[c]
+        for copy in back:
+            copy.wait_recv()
+        own.wait()
+
+        def blend(i, carry):
+            at = pl.ds(pl.multiple_of(c * chunk + i * narrow, narrow), narrow)
+            rows = returned[:, at]
+            branch = jnp.dot(mix_hi, rows, preferred_element_type=jnp.float32)
+            branch += jnp.dot(mix_lo, rows, preferred_element_type=jnp.float32)
+            tiles[0, :, at] = (tokens_ref[:, at].astype(jnp.float32) + branch).astype(jnp.bfloat16)
+            return carry
+
+        lax.fori_loop(0, chunk // narrow, blend, 0)
+        cols = pl.ds(c * chunk, chunk)
+        tile_sends.append(
+            (
+                tracked(tiles.at[0, :, cols], tiles.at[1, :, cols], to_x),
+                tracked(tiles.at[0, :, cols], tiles.at[2, :, cols], to_y),
+            )
+        )
+
+    def relay(c):
+        cols = pl.ds(c * chunk, chunk)
+        tile_x, tile_y = tile_sends[c]
+        tile_y.wait_recv()
+        tile_diag.append(tracked(tiles.at[2, top, cols], tiles.at[3, top, cols], to_x))
+        tile_x.wait_recv()
+        tile_diag.append(tracked(tiles.at[1, bottom, cols], tiles.at[3, bottom, cols], to_y))
+
+    shared = []
+
+    def share(slot, rows):
+        shared.append(tracked(key_buf.at[slot, rows, :], key_buf.at[slot, rows, :], to_sibling))
+
+    combine(0)
+    key_x, key_y = key_copies
+    key_y.wait_recv()
+    key_d0 = tracked(key_buf.at[2, quarter0, :], key_buf.at[3, quarter0, :], to_x)
+    share(2, my_half)
+    key_x.wait_recv()
+    key_d1 = tracked(key_buf.at[1, quarter1, :], key_buf.at[3, quarter1, :], to_y)
+    share(1, my_half)
+    combine(1)
+    relay(0)
+    combine(2)
+    relay(1)
+    key_d0.wait_recv()
+    share(3, quarter0)
+    key_d1.wait_recv()
+    share(3, quarter1)
+    combine(3)
+    relay(2)
+    relay(3)
+    for copy in tile_diag:
+        copy.wait_recv()
+
+    def choose(i, squares):
+        at = pl.ds(pl.multiple_of(i * narrow, narrow), narrow)
+        rows = pick_ref[0, :, 0:1] * tiles[0, :, at].astype(jnp.float32)
+        for slot in range(1, 4):
+            rows += pick_ref[slot, :, 0:1] * tiles[slot, :, at].astype(jnp.float32)
+        student_ref[:, at] = rows.astype(jnp.bfloat16)
+        return squares + jnp.sum(rows * rows, axis=-1, keepdims=True)
+
+    squares = lax.fori_loop(0, width // narrow, choose, jnp.zeros((tok_dev, 1), jnp.float32))
+    scale = lax.rsqrt(squares / width + 1e-05)
+
+    def norm(i, carry):
+        at = pl.ds(pl.multiple_of(i * narrow, narrow), narrow)
+        rows = student_ref[:, at].astype(jnp.float32)
+        normed[:, at] = (rows * scale * gain_ref[:, at]).astype(jnp.bfloat16)
+        return carry
+
+    lax.fori_loop(0, width // narrow, norm, 0)
+    own_key.wait()
+    for copy in shared:
+        copy.wait_recv()
+    columns = [
+        normed[:, pl.ds(pl.multiple_of(owner * key_rows, key_rows), key_rows)]
+        for owner in (d, dx, dy, dd)
+    ]
+
+    def to_keys(i, carry):
+        at = pl.ds(pl.multiple_of(i * narrow, narrow), narrow)
+        total = jnp.dot(columns[0], key_buf[0, :, at], preferred_element_type=jnp.float32)
+        for slot in range(1, 4):
+            total += jnp.dot(columns[slot], key_buf[slot, :, at], preferred_element_type=jnp.float32)
+        keys_ref[:, at] = total.astype(jnp.bfloat16)
+        return carry
+
+    lax.fori_loop(0, key_width // narrow, to_keys, 0)
+    for copy in sent:
+        copy.wait_send()
+
+
+def fused(
+    tokens,
+    gate_proj,
+    up_proj,
+    down_proj,
+    route_ids,
+    route_slots,
+    route_gates,
+    image_shard,
+    norm_gain,
+    key_proj,
+    capacity,
+):
+    tok_dev, width = tokens.shape
+    n_expert = lax.axis_size("expert")
+    slots = n_expert * capacity
+    units = gate_proj.shape[1]
+    key_rows, key_width = key_proj.shape
+    retained = route_slots < capacity
+    cells = jnp.where(retained, route_ids * capacity + route_slots, slots)
+    grid = jnp.arange(slots, dtype=jnp.int32)
+    spread = jnp.any(cells.T[:, None, :] == grid[None, :, None], axis=0).astype(jnp.bfloat16)
+    mix = jnp.sum(
+        jnp.where(cells[:, :, None] == grid[None, None, :], route_gates[:, :, None], 0.0), axis=1
+    )
+    d = lax.axis_index("dp")
+    dx = d + 1 - 2 * (d % 2)
+    order = jnp.stack([d, dx, (d + 2) % 4, (dx + 2) % 4])
+    pick = (jnp.take(image_shard.reshape(-1), order) == d).astype(jnp.float32)
+    pick = jnp.broadcast_to(pick[:, None, None], (4, tok_dev, 128))
+    remote = 8 + (n_expert - 1) * (1 + CHUNKS) + 4 * CHUNKS * 2 + 8
+    vmem = pl.BlockSpec(memory_space=pltpu.VMEM)
+    anywhere = pl.BlockSpec(memory_space=pl.ANY)
+    half = jnp.bfloat16
+    return pl.pallas_call(
+        functools.partial(fused_kernel, n_expert, capacity),
+        out_shape=(
+            jax.ShapeDtypeStruct((tok_dev, width), half),
+            jax.ShapeDtypeStruct((tok_dev, key_width), half),
+        ),
+        in_specs=[vmem] * 5 + [anywhere] * 4,
+        out_specs=(vmem, vmem),
+        scratch_shapes=[
+            pltpu.VMEM((4, units, width), half),
+            pltpu.VMEM((4, units, width), half),
+            pltpu.VMEM((4, units, width), half),
+            pltpu.VMEM((4, key_rows, key_width), half),
+            pltpu.VMEM((slots, width), half),
+            pltpu.VMEM((slots, width), half),
+            pltpu.VMEM((slots, width), half),
+            pltpu.VMEM((slots, width), half),
+            pltpu.VMEM((4, tok_dev, width), half),
+            pltpu.VMEM((4, slots, units), half),
+            pltpu.VMEM((tok_dev, width), half),
+            pltpu.VMEM((slots, units), jnp.float32),
+            pltpu.VMEM((slots, units), jnp.float32),
+            pltpu.SemaphoreType.DMA((remote,)),
+            pltpu.SemaphoreType.DMA((remote,)),
+            pltpu.SemaphoreType.DMA((5 + CHUNKS,)),
+        ],
+        compiler_params=pltpu.CompilerParams(
+            collective_id=0, has_side_effects=True, vmem_limit_bytes=60 * 1024 * 1024
+        ),
+    )(
+        spread,
+        mix,
+        pick,
+        norm_gain.reshape(1, -1),
+        tokens,
+        gate_proj,
+        up_proj,
+        down_proj,
+        key_proj,
+    )
 
 
 def per_device(
@@ -35,6 +428,21 @@
     top_count = route_ids.shape[1]
     experts = gate_proj.shape[0] * lax.axis_size("expert")
     capacity = 3 * tok_dev * top_count // (2 * experts)
+    if capacity % 16 == 0 and gate_proj.shape[0] == 1 and lax.axis_size("dp") == 4:
+        if tok_dev == IMG_TOK and gate_proj.shape[1] % 32 == 0 and key_proj.shape[0] % 128 == 0:
+            return fused(
+                tokens,
+                gate_proj,
+                up_proj,
+                down_proj,
+                route_ids,
+                route_slots,
+                route_gates,
+                image_shard,
+                norm_gain,
+                key_proj,
+                capacity,
+            )
     slot_total = experts * capacity
     retained = route_slots < capacity
     slot_cells = jnp.where(retained, route_ids * capacity + route_slots, slot_total).reshape(-1)

time: 444 us -> 250 us (0.56)
  waiting for transfers between devices: 280 us -> 0 us
  Pallas kernels: 0 us -> 241 us
  blocking collectives: 77.8 us -> 0 us
  matrix products: 28.3 us -> 0 us
  local copies, waits for them, and re-layouts: 27.3 us -> 5.08 us
  between operations: 14 us -> 0.71 us
  other arithmetic: 11.3 us -> 3.06 us
  starting transfers between devices: 5.11 us -> 0 us
    pallas_call x0 -> x1, Pallas kernels: none -> 241 us  [fused(): pl.pallas_call(functools.partial(fused_kernel, n_expert, capacity), out_s...]
    all_gather x4 -> x0, waiting for transfers between devices: 174 us -> none  [the longest x1 71.9 us: per_device(): lax.all_gather(down_proj, 'dp', axis=1, tiled=True)[0]]
    all_to_all x1 -> x0, blocking collectives: 77.8 us -> none  [per_device(): lax.all_to_all(outgoing, 'expert', split_axis=0, concat_axis=0, tiled=True)]
    all_to_all x1 -> x0, waiting for transfers between devices: 71.1 us -> none  [per_device(): lax.all_to_all(produced, 'expert', split_axis=0, concat_axis=0, tiled=True)]
    reduce_scatter x1 -> x0, waiting for transfers between devices: 33 us -> none  [per_device(): lax.psum_scatter(jnp.dot(columns, key_proj, preferred_element_type=jnp.fl...]
    dot_general x4 -> x0, matrix products: 28.3 us -> none  [the longest x1 14.2 us: per_device(): jnp.dot(hidden, lax.all_gather(down_proj, 'dp', axis=1, tiled=True)[0], p...]
    gather x4 -> x1, local copies, waits for them, and re-layouts: 20.9 us -> 0.64 us  [fused(): pick = (jnp.take(image_shard.reshape(-1), order) == d).astype(jnp.float32)]
    all_to_all x1 -> x0, starting transfers between devices: 4.74 us -> none  [per_device(): lax.all_to_all(produced, 'expert', split_axis=0, concat_axis=0, tiled=True)]
  transfers between devices with their start and end apart: 6 -> 0, of which waited for: 5 -> 0; matrix products, arithmetic and copies ran while one was open for 4% -> 0% of each run, Pallas kernels for 0% -> 0%
where the time goes in v1:
time: 250 us; the launch traced here: 249 us
  Pallas kernels  241 us (96%)
  local copies, waits for them, and re-layouts  5.08 us (2%)
  other arithmetic  3.06 us (1%)
    pallas_call x1, Pallas kernels, fused(): pl.pallas_call(functools.partial(fused_kernel, n_expert, capacity), out_s...  241 us

profile of v1, /device:TPU:0, one launch (start us, length us, event | category | flops | bytes accessed | tf_op | source)
XLA Modules:
  0.0 249.5 jit_solution(8363861065255340362)
XLA Ops:
  0.6 0.0 copy-start
  0.7 0.6 copy-done
  1.3 0.1 fusion.1
  1.4 0.7 compare_select_fusion.2
  2.1 0.6 gather_fusion
  2.7 0.1 compare_convert_fusion
  2.9 0.6 convert_element_type.10.spread_ref
  3.5 1.5 select_reduce_fusion.mix_ref
  5.0 0.8 broadcast_in_dim.32.pick_ref
  5.8 240.6 %shard_map.113 = (bf16[128,4096]{1,0:T(8,128)(2,1)}, bf16[128,1024]{1,0:T(8,128)(2,1)}) custom-call(bf16[384,128]{1,0:T(8,128)(2,1)} %convert_element_type.10.spread_ref, f32[128,384]{1,0:T(8,128)} %select_reduce_fusion.mix_ref, f32[4,128,128]{2,1,0:T(8,128)} %broadcast_in_dim.32.pick_ref, f32[1,4096]{1,0:T(1,128)} %bitcast.14, ...), custom_call_target="tpu_custom_call" | custom-call | tf_op jit(solution)/shard_map/pallas_call | solution.py:373
  246.4 0.0 copy-start.1
  246.4 2.3 copy.18
  248.7 0.0 copy-done.1
  248.8 0.7 copy.19
  (2 shorter events, 0.0 us)
Async XLA Ops:
  0.6 0.7 copy-start
  246.4 2.3 copy-start.1

commit v2 on v1

--- a/solution.py
+++ b/solution.py
@@ -23,16 +23,19 @@
     return (jax.nn.silu(gate_act) * up_act).astype(jnp.bfloat16)
 
 
-CHUNKS = 4
+CHUNKS = 8
+PIECES = 2
+LAG = 3
 MESH = pl.DeviceIdType.MESH
 
 
 def fused_kernel(
     n_expert,
     capacity,
-    spread_ref,
-    mix_ref,
-    pick_ref,
+    ids_ref,
+    slots_ref,
+    gates_ref,
+    shard_ref,
     gain_ref,
     tokens_ref,
     gate_ref,
@@ -50,10 +53,14 @@
     produced,
     returned,
     tiles,
+    passed,
     hidden,
-    normed,
+    gained,
+    mixing,
+    acc_keys,
     acc_gate,
     acc_up,
+    squares,
     send_sem,
     recv_sem,
     local_sem,
@@ -65,13 +72,16 @@
     dd = (dx + 2) % 4
     core = e % 2
     sibling = e + 1 - 2 * core
+    partner = e + 2 - 4 * ((e // 2) % 2)
     tok_dev, width = tokens_ref.shape
     units = gate_ref.shape[1]
     half_units = units // 2
     chunk = width // CHUNKS
     key_rows, key_width = key_ref.shape
-    key_half = key_rows // 2
-    key_quarter = key_rows // 4
+    quarter = key_rows // 4
+    piece = quarter // PIECES
+    half_piece = piece // 2
+    slots = n_expert * capacity
     counts = {"remote": 0, "local": 0}
 
     def send(source, target, where):
@@ -96,6 +106,7 @@
         return copy
 
     to_x, to_y, to_sibling = {"dp": dx}, {"dp": dy}, {"expert": sibling}
+    to_partner = {"expert": partner}
     peers = [lax.rem(e + k, n_expert) for k in range(1, n_expert)]
     barrier = pltpu.get_barrier_semaphore()
     for where in [to_x, to_y] + [{"expert": peer} for peer in peers]:
@@ -115,10 +126,20 @@
     own_gate = local(gate_ref.at[0], gate_buf.at[0])
     own_up = local(up_ref.at[0], up_buf.at[0])
     own_down = local(down_ref.at[0], down_buf.at[0])
-    own_key = local(key_ref, key_buf.at[0])
+    own_key = local(key_ref, key_buf.at[d])
 
     step = 512
-    spread = spread_ref[...]
+    grid = lax.broadcasted_iota(jnp.int32, (tok_dev, slots), 1)
+    mix = jnp.zeros((tok_dev, slots), jnp.float32)
+    named = jnp.zeros((tok_dev, slots), jnp.float32)
+    for k in range(ids_ref.shape[1]):
+        queue = slots_ref[:, k : k + 1]
+        cell = jnp.where(queue < capacity, ids_ref[:, k : k + 1] * capacity + queue, slots)
+        hit = grid == cell
+        mix += jnp.where(hit, gates_ref[:, k : k + 1], 0.0)
+        named += jnp.where(hit, 1.0, 0.0)
+    mixing[...] = mix
+    spread = named.T.astype(jnp.bfloat16)
 
     def fill(i, carry):
         cols = pl.ds(pl.multiple_of(i * step, step), step)
@@ -155,7 +176,60 @@
             tracked(down_ref.at[0, :, cols], down_buf.at[2, :, cols], to_y),
         )
 
+    def key_rows_at(owner, p, start=0, size=piece):
+        first = (owner % 4) * quarter + p * piece + start
+        return pl.ds(pl.multiple_of(first, half_piece), size)
+
+    def key_own(p):
+        rows = key_rows_at(e, p)
+        return (
+            tracked(key_ref.at[rows, :], key_buf.at[d, rows, :], to_x),
+            tracked(key_ref.at[rows, :], key_buf.at[d, rows, :], to_y),
+        )
+
+    key_first, key_second, key_across, key_shared = [], [], [], []
+
+    def pass_key(owner, rows, where):
+        part = key_buf.at[owner, rows, :]
+        return tracked(part, part, where)
+
+    def key_share(owner, rows):
+        key_across.append(pass_key(owner, rows, to_partner))
+        key_shared.append(pass_key(owner, rows, to_sibling))
+
+    def key_middle(p):
+        key_x, key_y = key_first[p]
+        rows = key_rows_at(e, p)
+        key_y.wait_recv()
+        d0 = pass_key(dy, key_rows_at(e, p, 0, half_piece), to_x)
+        key_x.wait_recv()
+        d1 = pass_key(dx, key_rows_at(e, p, half_piece, half_piece), to_y)
+        key_second.append((d0, d1))
+        key_share(dy, rows)
+        key_share(dx, rows)
+
+    def key_diagonal(p):
+        d0, d1 = key_second[p]
+        d0.wait_recv()
+        key_share(dd, key_rows_at(e, p, 0, half_piece))
+        d1.wait_recv()
+        key_share(dd, key_rows_at(e, p, half_piece, half_piece))
+
+    def key_onward(p, halves):
+        copies = key_across[4 * p + 2 * halves : 4 * p + 2 * halves + 2]
+        if halves:
+            places = [
+                (dd, key_rows_at(partner, p, 0, half_piece)),
+                (dd, key_rows_at(partner, p, half_piece, half_piece)),
+            ]
+        else:
+            places = [(dy, key_rows_at(partner, p)), (dx, key_rows_at(partner, p))]
+        for copy, (owner, rows) in zip(copies, places):
+            copy.wait_recv()
+            key_shared.append(pass_key(owner, rows, to_sibling))
+
     downs = [down_own(0), down_own(1)]
+    key_first.append(key_own(0))
 
     for copy in dispatched:
         copy.wait_recv()
@@ -195,10 +269,88 @@
 
     narrow = 256
     hands = []
-    key_copies = []
-    my_half = pl.ds(pl.multiple_of(core * key_half, key_half), key_half)
-    quarter0 = pl.ds(pl.multiple_of(core * key_half, key_quarter), key_quarter)
-    quarter1 = pl.ds(pl.multiple_of(core * key_half + key_quarter, key_quarter), key_quarter)
+    tile_first, tile_second = [], []
+    acc_keys[...] = jnp.zeros_like(acc_keys)
+    squares[...] = jnp.zeros_like(squares)
+
+    def flag(owner, shard):
+        return jnp.where(shard_ref[owner, 0] == shard, 1.0, 0.0)
+
+    def ways(c):
+        return (dx, dy, to_x, to_y) if c % 2 == 0 else (dy, dx, to_y, to_x)
+
+    def combine(c):
+        back, own = hands[c]
+        for copy in back:
+            copy.wait_recv()
+        own.wait()
+        mix = mixing[...]
+        mix_hi = mix.astype(jnp.bfloat16)
+        mix_lo = (mix - mix_hi.astype(jnp.float32)).astype(jnp.bfloat16)
+
+        def blend(i, carry):
+            at = pl.ds(pl.multiple_of(c * chunk + i * narrow, narrow), narrow)
+            rows = returned[:, at]
+            branch = jnp.dot(mix_hi, rows, preferred_element_type=jnp.float32)
+            branch += jnp.dot(mix_lo, rows, preferred_element_type=jnp.float32)
+            tiles[0, :, at] = (tokens_ref[:, at].astype(jnp.float32) + branch).astype(jnp.bfloat16)
+            return carry
+
+        lax.fori_loop(0, chunk // narrow, blend, 0)
+        cols = pl.ds(c * chunk, chunk)
+        tile_first.append(tracked(tiles.at[0, :, cols], tiles.at[1, :, cols], ways(c)[2]))
+
+    def swap(c):
+        near, far, _, to_far = ways(c)
+        own = flag(d, far)
+        tile_first[c].wait_recv()
+
+        def mask(i, carry):
+            at = pl.ds(pl.multiple_of(c * chunk + i * narrow, narrow), narrow)
+            rows = own * tiles[0, :, at].astype(jnp.float32)
+            rows += (1.0 - own) * tiles[1, :, at].astype(jnp.float32)
+            passed[:, at] = rows.astype(jnp.bfloat16)
+            return carry
+
+        lax.fori_loop(0, chunk // narrow, mask, 0)
+        cols = pl.ds(c * chunk, chunk)
+        tile_second.append(tracked(passed.at[:, cols], tiles.at[2, :, cols], to_far))
+
+    def finish(c):
+        near = ways(c)[0]
+        weights = [flag(d, d), flag(near, d)]
+        weights.append(1.0 - weights[0] - weights[1])
+        tile_second[c].wait_recv()
+
+        def choose(i, carry):
+            at = pl.ds(pl.multiple_of(c * chunk + i * narrow, narrow), narrow)
+            rows = weights[0] * tiles[0, :, at].astype(jnp.float32)
+            for slot in (1, 2):
+                rows += weights[slot] * tiles[slot, :, at].astype(jnp.float32)
+            student_ref[:, at] = rows.astype(jnp.bfloat16)
+            gained[:, at] = (rows * gain_ref[:, at]).astype(jnp.bfloat16)
+            squares[...] += jnp.sum(rows * rows, axis=-1, keepdims=True)
+            return carry
+
+        lax.fori_loop(0, chunk // narrow, choose, 0)
+
+    def project_keys(c, carry):
+        at = pl.ds(pl.multiple_of(c * chunk, chunk), chunk)
+        per_owner = key_rows // chunk
+        rows = pl.ds(pl.multiple_of((c % per_owner) * chunk, chunk), chunk)
+        acc_keys[...] += jnp.dot(
+            gained[:, at], key_buf[c // per_owner, rows, :], preferred_element_type=jnp.float32
+        )
+        return carry
+
+    def follow(c):
+        if 0 <= c - LAG < CHUNKS:
+            combine(c - LAG)
+        if 0 <= c - LAG - 1 < CHUNKS:
+            swap(c - LAG - 1)
+        if 0 <= c - LAG - 2 < CHUNKS:
+            finish(c - LAG - 2)
+
     for c in range(CHUNKS):
         cols = pl.ds(c * chunk, chunk)
         down_x, down_y = downs[c]
@@ -208,9 +360,8 @@
         d1 = tracked(down_buf.at[1, high, cols], down_buf.at[3, high, cols], to_y)
         if c + 2 < CHUNKS:
             downs.append(down_own(c + 2))
-        elif c + 1 == CHUNKS:
-            key_copies.append(tracked(key_ref.at[my_half, :], key_buf.at[1, my_half, :], to_x))
-            key_copies.append(tracked(key_ref.at[my_half, :], key_buf.at[2, my_half, :], to_y))
+        if c == 1:
+            key_first.append(key_own(1))
         d0.wait_recv()
         d1.wait_recv()
 
@@ -231,107 +382,31 @@
         ]
         hands.append((back, local(produced.at[mine, cols], returned.at[mine, cols])))
 
-    mix = mix_ref[...]
-    mix_hi = mix.astype(jnp.bfloat16)
-    mix_lo = (mix - mix_hi.astype(jnp.float32)).astype(jnp.bfloat16)
-    half_tok = tok_dev // 2
-    top, bottom = pl.ds(0, half_tok), pl.ds(half_tok, half_tok)
-    tile_sends = []
-    tile_diag = []
-
-    def combine(c):
-        back, own = hands[c]
-        for copy in back:
-            copy.wait_recv()
-        own.wait()
-
-        def blend(i, carry):
-            at = pl.ds(pl.multiple_of(c * chunk + i * narrow, narrow), narrow)
-            rows = returned[:, at]
-            branch = jnp.dot(mix_hi, rows, preferred_element_type=jnp.float32)
-            branch += jnp.dot(mix_lo, rows, preferred_element_type=jnp.float32)
-            tiles[0, :, at] = (tokens_ref[:, at].astype(jnp.float32) + branch).astype(jnp.bfloat16)
-            return carry
-
-        lax.fori_loop(0, chunk // narrow, blend, 0)
-        cols = pl.ds(c * chunk, chunk)
-        tile_sends.append(
-            (
-                tracked(tiles.at[0, :, cols], tiles.at[1, :, cols], to_x),
-                tracked(tiles.at[0, :, cols], tiles.at[2, :, cols], to_y),
-            )
-        )
-
-    def relay(c):
-        cols = pl.ds(c * chunk, chunk)
-        tile_x, tile_y = tile_sends[c]
-        tile_y.wait_recv()
-        tile_diag.append(tracked(tiles.at[2, top, cols], tiles.at[3, top, cols], to_x))
-        tile_x.wait_recv()
-        tile_diag.append(tracked(tiles.at[1, bottom, cols], tiles.at[3, bottom, cols], to_y))
-
-    shared = []
-
-    def share(slot, rows):
-        shared.append(tracked(key_buf.at[slot, rows, :], key_buf.at[slot, rows, :], to_sibling))
-
-    combine(0)
-    key_x, key_y = key_copies
-    key_y.wait_recv()
-    key_d0 = tracked(key_buf.at[2, quarter0, :], key_buf.at[3, quarter0, :], to_x)
-    share(2, my_half)
-    key_x.wait_recv()
-    key_d1 = tracked(key_buf.at[1, quarter1, :], key_buf.at[3, quarter1, :], to_y)
-    share(1, my_half)
-    combine(1)
-    relay(0)
-    combine(2)
-    relay(1)
-    key_d0.wait_recv()
-    share(3, quarter0)
-    key_d1.wait_recv()
-    share(3, quarter1)
-    combine(3)
-    relay(2)
-    relay(3)
-    for copy in tile_diag:
+        if c == 2:
+            key_middle(0)
+        if c == 4:
+            key_diagonal(0)
+            key_middle(1)
+        if c == 6:
+            key_diagonal(1)
+            key_onward(0, 0)
+        follow(c)
+
+    key_onward(0, 1)
+    key_onward(1, 0)
+    follow(CHUNKS)
+    key_onward(1, 1)
+    follow(CHUNKS + 1)
+    own_key.wait()
+    for copy in key_shared:
         copy.wait_recv()
-
-    def choose(i, squares):
-        at = pl.ds(pl.multiple_of(i * narrow, narrow), narrow)
-        rows = pick_ref[0, :, 0:1] * tiles[0, :, at].astype(jnp.float32)
-        for slot in range(1, 4):
-            rows += pick_ref[slot, :, 0:1] * tiles[slot, :, at].astype(jnp.float32)
-        student_ref[:, at] = rows.astype(jnp.bfloat16)
-        return squares + jnp.sum(rows * rows, axis=-1, keepdims=True)
-
-    squares = lax.fori_loop(0, width // narrow, choose, jnp.zeros((tok_dev, 1), jnp.float32))
-    scale = lax.rsqrt(squares / width + 1e-05)
-
-    def norm(i, carry):
-        at = pl.ds(pl.multiple_of(i * narrow, narrow), narrow)
-        rows = student_ref[:, at].astype(jnp.float32)
-        normed[:, at] = (rows * scale * gain_ref[:, at]).astype(jnp.bfloat16)
-        return carry
-
-    lax.fori_loop(0, width // narrow, norm, 0)
-    own_key.wait()
-    for copy in shared:
-        copy.wait_recv()
-    columns = [
-        normed[:, pl.ds(pl.multiple_of(owner * key_rows, key_rows), key_rows)]
-        for owner in (d, dx, dy, dd)
-    ]
-
-    def to_keys(i, carry):
-        at = pl.ds(pl.multiple_of(i * narrow, narrow), narrow)
-        total = jnp.dot(columns[0], key_buf[0, :, at], preferred_element_type=jnp.float32)
-        for slot in range(1, 4):
-            total += jnp.dot(columns[slot], key_buf[slot, :, at], preferred_element_type=jnp.float32)
-        keys_ref[:, at] = total.astype(jnp.bfloat16)
-        return carry
-
-    lax.fori_loop(0, key_width // narrow, to_keys, 0)
+    ready = CHUNKS + 2 - LAG - 2
+    lax.fori_loop(0, ready, project_keys, 0)
+    for c in range(CHUNKS + 2, CHUNKS + LAG + 2):
+        follow(c)
+        project_keys(c - LAG - 2, 0)
+    scale = lax.rsqrt(squares[...] / width + 1e-05)
+    keys_ref[...] = (acc_keys[...] * scale).astype(jnp.bfloat16)
     for copy in sent:
         copy.wait_send()
 
@@ -354,21 +429,10 @@
     slots = n_expert * capacity
     units = gate_proj.shape[1]
     key_rows, key_width = key_proj.shape
-    retained = route_slots < capacity
-    cells = jnp.where(retained, route_ids * capacity + route_slots, slots)
-    grid = jnp.arange(slots, dtype=jnp.int32)
-    spread = jnp.any(cells.T[:, None, :] == grid[None, :, None], axis=0).astype(jnp.bfloat16)
-    mix = jnp.sum(
-        jnp.where(cells[:, :, None] == grid[None, None, :], route_gates[:, :, None], 0.0), axis=1
-    )
-    d = lax.axis_index("dp")
-    dx = d + 1 - 2 * (d % 2)
-    order = jnp.stack([d, dx, (d + 2) % 4, (dx + 2) % 4])
-    pick = (jnp.take(image_shard.reshape(-1), order) == d).astype(jnp.float32)
-    pick = jnp.broadcast_to(pick[:, None, None], (4, tok_dev, 128))
-    remote = 8 + (n_expert - 1) * (1 + CHUNKS) + 4 * CHUNKS * 2 + 8
+    remote = 8 + 16 * PIECES + (n_expert - 1) * (1 + CHUNKS) + 6 * CHUNKS
     vmem = pl.BlockSpec(memory_space=pltpu.VMEM)
     anywhere = pl.BlockSpec(memory_space=pl.ANY)
+    scalars = pl.BlockSpec(memory_space=pltpu.SMEM)
     half = jnp.bfloat16
     return pl.pallas_call(
         functools.partial(fused_kernel, n_expert, capacity),
@@ -376,7 +440,7 @@
             jax.ShapeDtypeStruct((tok_dev, width), half),
             jax.ShapeDtypeStruct((tok_dev, key_width), half),
         ),
-        in_specs=[vmem] * 5 + [anywhere] * 4,
+        in_specs=[vmem] * 3 + [scalars] + [vmem] * 2 + [anywhere] * 4,
         out_specs=(vmem, vmem),
         scratch_shapes=[
             pltpu.VMEM((4, units, width), half),
@@ -387,11 +451,15 @@
             pltpu.VMEM((slots, width), half),
             pltpu.VMEM((slots, width), half),
             pltpu.VMEM((slots, width), half),
-            pltpu.VMEM((4, tok_dev, width), half),
+            pltpu.VMEM((3, tok_dev, width), half),
+            pltpu.VMEM((tok_dev, width), half),
             pltpu.VMEM((4, slots, units), half),
             pltpu.VMEM((tok_dev, width), half),
+            pltpu.VMEM((tok_dev, slots), jnp.float32),
+            pltpu.VMEM((tok_dev, key_width), jnp.float32),
             pltpu.VMEM((slots, units), jnp.float32),
             pltpu.VMEM((slots, units), jnp.float32),
+            pltpu.VMEM((tok_dev, 1), jnp.float32),
             pltpu.SemaphoreType.DMA((remote,)),
             pltpu.SemaphoreType.DMA((remote,)),
             pltpu.SemaphoreType.DMA((5 + CHUNKS,)),
@@ -400,9 +468,10 @@
             collective_id=0, has_side_effects=True, vmem_limit_bytes=60 * 1024 * 1024
         ),
     )(
-        spread,
-        mix,
-        pick,
+        route_ids,
+        route_slots,
+        route_gates,
+        image_shard,
         norm_gain.reshape(1, -1),
         tokens,
         gate_proj,
@@ -428,8 +497,8 @@
     top_count = route_ids.shape[1]
     experts = gate_proj.shape[0] * lax.axis_size("expert")
     capacity = 3 * tok_dev * top_count // (2 * experts)
-    if capacity % 16 == 0 and gate_proj.shape[0] == 1 and lax.axis_size("dp") == 4:
-        if tok_dev == IMG_TOK and gate_proj.shape[1] % 32 == 0 and key_proj.shape[0] % 128 == 0:
+    if capacity % 16 == 0 and gate_proj.shape[0] == 1 and lax.axis_size("dp") == 4 and experts % 4 == 0:
+        if tok_dev == IMG_TOK and gate_proj.shape[1] % 32 == 0 and key_proj.shape[0] % 512 == 0:
             return fused(
                 tokens,
                 gate_proj,

time: 250 us -> 244 us (0.976)
  Pallas kernels: 241 us -> 234 us
  local copies, waits for them, and re-layouts: 5.08 us -> 8.59 us
  other arithmetic: 3.06 us -> 0 us
    pallas_call x1, Pallas kernels: 241 us -> 234 us  [fused(): pl.pallas_call(functools.partial(fused_kernel, n_expert, capacity), out_s...]
    unnamed x6 -> x8, local copies, waits for them, and re-layouts: 3.65 us -> 8.59 us
where the time goes in v2:
time: 244 us; the launch traced here: 243 us
  Pallas kernels  234 us (96%)
  local copies, waits for them, and re-layouts  8.59 us (4%)
    pallas_call x1, Pallas kernels, fused(): pl.pallas_call(functools.partial(fused_kernel, n_expert, capacity), out_s...  234 us
    unnamed x8, local copies, waits for them, and re-layouts  8.59 us

profile of v2, /device:TPU:0, one launch (start us, length us, event | category | flops | bytes accessed | tf_op | source)
XLA Modules:
  0.0 243.3 jit_solution(9246417447868001691)
XLA Ops:
  0.6 1.3 copy.15.shard_ref
  2.0 1.4 copy.12.ids_ref
  3.4 1.4 copy.13.slots_ref
  4.8 1.4 copy.14.gates_ref
  6.2 234.0 %shard_map.113 = (bf16[128,4096]{1,0:T(8,128)(2,1)}, bf16[128,1024]{1,0:T(8,128)(2,1)}) custom-call(s32[128,2]{1,0:T(8,128)} %copy.12.ids_ref, s32[128,2]{1,0:T(8,128)} %copy.13.slots_ref, f32[128,2]{1,0:T(8,128)} %copy.14.gates_ref, s32[4,1]{1,0:T(4,128)} %copy.15.shard_ref, f32[1,4096]{1,0:T(1,128)} %bitcast.1, bf16[128,4096]{1,0:T(8,128)(2,1)} %tokens_ref.1, ...), custom_call_target="tpu_custom_call" | custom-call | tf_op jit(solution)/shard_map/pallas_call | solution.py:437
  240.2 0.0 copy-start
  240.2 2.3 copy.18
  242.6 0.0 copy-done
  242.6 0.7 copy.19
Async XLA Ops:
  240.2 2.3 copy-start

commit v3 on v2

--- a/solution.py
+++ b/solution.py
@@ -23,9 +23,9 @@
     return (jax.nn.silu(gate_act) * up_act).astype(jnp.bfloat16)
 
 
-CHUNKS = 8
+CHUNKS = 4
 PIECES = 2
-LAG = 3
+LAG = 2
 MESH = pl.DeviceIdType.MESH
 
 
@@ -72,14 +72,13 @@
     dd = (dx + 2) % 4
     core = e % 2
     sibling = e + 1 - 2 * core
-    partner = e + 2 - 4 * ((e // 2) % 2)
     tok_dev, width = tokens_ref.shape
     units = gate_ref.shape[1]
     half_units = units // 2
     chunk = width // CHUNKS
     key_rows, key_width = key_ref.shape
-    quarter = key_rows // 4
-    piece = quarter // PIECES
+    key_half = key_rows // 2
+    piece = key_half // PIECES
     half_piece = piece // 2
     slots = n_expert * capacity
     counts = {"remote": 0, "local": 0}
@@ -106,7 +105,6 @@
         return copy
 
     to_x, to_y, to_sibling = {"dp": dx}, {"dp": dy}, {"expert": sibling}
-    to_partner = {"expert": partner}
     peers = [lax.rem(e + k, n_expert) for k in range(1, n_expert)]
     barrier = pltpu.get_barrier_semaphore()
     for where in [to_x, to_y] + [{"expert": peer} for peer in peers]:
@@ -177,7 +175,7 @@
         )
 
     def key_rows_at(owner, p, start=0, size=piece):
-        first = (owner % 4) * quarter + p * piece + start
+        first = (owner % 2) * key_half + p * piece + start
         return pl.ds(pl.multiple_of(first, half_piece), size)
 
     def key_own(p):
@@ -187,14 +185,13 @@
             tracked(key_ref.at[rows, :], key_buf.at[d, rows, :], to_y),
         )
 
-    key_first, key_second, key_across, key_shared = [], [], [], []
+    key_first, key_second, key_shared = [], [], []
 
     def pass_key(owner, rows, where):
         part = key_buf.at[owner, rows, :]
         return tracked(part, part, where)
 
     def key_share(owner, rows):
-        key_across.append(pass_key(owner, rows, to_partner))
         key_shared.append(pass_key(owner, rows, to_sibling))
 
     def key_middle(p):
@@ -215,21 +212,7 @@
         d1.wait_recv()
         key_share(dd, key_rows_at(e, p, half_piece, half_piece))
 
-    def key_onward(p, halves):
-        copies = key_across[4 * p + 2 * halves : 4 * p + 2 * halves + 2]
-        if halves:
-            places = [
-                (dd, key_rows_at(partner, p, 0, half_piece)),
-                (dd, key_rows_at(partner, p, half_piece, half_piece)),
-            ]
-        else:
-            places = [(dy, key_rows_at(partner, p)), (dx, key_rows_at(partner, p))]
-        for copy, (owner, rows) in zip(copies, places):
-            copy.wait_recv()
-            key_shared.append(pass_key(owner, rows, to_sibling))
-
     downs = [down_own(0), down_own(1)]
-    key_first.append(key_own(0))
 
     for copy in dispatched:
         copy.wait_recv()
@@ -360,8 +343,8 @@
         d1 = tracked(down_buf.at[1, high, cols], down_buf.at[3, high, cols], to_y)
         if c + 2 < CHUNKS:
             downs.append(down_own(c + 2))
-        if c == 1:
-            key_first.append(key_own(1))
+        elif c + 1 == CHUNKS:
+            key_first.extend(key_own(p) for p in range(PIECES))
         d0.wait_recv()
         d1.wait_recv()
 
@@ -382,21 +365,14 @@
         ]
         hands.append((back, local(produced.at[mine, cols], returned.at[mine, cols])))
 
-        if c == 2:
-            key_middle(0)
-        if c == 4:
-            key_diagonal(0)
-            key_middle(1)
-        if c == 6:
-            key_diagonal(1)
-            key_onward(0, 0)
         follow(c)
 
-    key_onward(0, 1)
-    key_onward(1, 0)
     follow(CHUNKS)
-    key_onward(1, 1)
+    for p in range(PIECES):
+        key_middle(p)
     follow(CHUNKS + 1)
+    for p in range(PIECES):
+        key_diagonal(p)
     own_key.wait()
     for copy in key_shared:
         copy.wait_recv()
@@ -429,7 +405,7 @@
     slots = n_expert * capacity
     units = gate_proj.shape[1]
     key_rows, key_width = key_proj.shape
-    remote = 8 + 16 * PIECES + (n_expert - 1) * (1 + CHUNKS) + 6 * CHUNKS
+    remote = 8 + 8 * PIECES + (n_expert - 1) * (1 + CHUNKS) + 6 * CHUNKS
     vmem = pl.BlockSpec(memory_space=pltpu.VMEM)
     anywhere = pl.BlockSpec(memory_space=pl.ANY)
     scalars = pl.BlockSpec(memory_space=pltpu.SMEM)
@@ -497,7 +473,7 @@
     top_count = route_ids.shape[1]
     experts = gate_proj.shape[0] * lax.axis_size("expert")
     capacity = 3 * tok_dev * top_count // (2 * experts)
-    if capacity % 16 == 0 and gate_proj.shape[0] == 1 and lax.axis_size("dp") == 4 and experts % 4 == 0:
+    if capacity % 16 == 0 and gate_proj.shape[0] == 1 and lax.axis_size("dp") == 4 and experts % 2 == 0:
         if tok_dev == IMG_TOK and gate_proj.shape[1] % 32 == 0 and key_proj.shape[0] % 512 == 0:
             return fused(
                 tokens,

time: 244 us -> 239 us (0.980)
  Pallas kernels: 234 us -> 230 us
    pallas_call x1, Pallas kernels: 234 us -> 230 us  [fused(): pl.pallas_call(functools.partial(fused_kernel, n_expert, capacity), out_s...]
where the time goes in v3:
time: 239 us
  Pallas kernels  230 us (96%)
  local copies, waits for them, and re-layouts  8.59 us (4%)
    pallas_call x1, Pallas kernels, fused(): pl.pallas_call(functools.partial(fused_kernel, n_expert, capacity), out_s...  230 us
    unnamed x8, local copies, waits for them, and re-layouts  8.59 us

profile of v3, /device:TPU:0, one launch (start us, length us, event | category | flops | bytes accessed | tf_op | source)
XLA Modules:
  0.0 238.8 jit_solution(16303405332051800898)
XLA Ops:
  0.6 1.3 copy.15.shard_ref
  2.0 1.4 copy.12.ids_ref
  3.4 1.4 copy.13.slots_ref
  4.8 1.4 copy.14.gates_ref
  6.2 229.6 %shard_map.113 = (bf16[128,4096]{1,0:T(8,128)(2,1)}, bf16[128,1024]{1,0:T(8,128)(2,1)}) custom-call(s32[128,2]{1,0:T(8,128)} %copy.12.ids_ref, s32[128,2]{1,0:T(8,128)} %copy.13.slots_ref, f32[128,2]{1,0:T(8,128)} %copy.14.gates_ref, s32[4,1]{1,0:T(4,128)} %copy.15.shard_ref, f32[1,4096]{1,0:T(1,128)} %bitcast.1, bf16[128,4096]{1,0:T(8,128)(2,1)} %tokens_ref.1, ...), custom_call_target="tpu_custom_call" | custom-call | tf_op jit(solution)/shard_map/pallas_call | solution.py:413
  235.8 0.0 copy-start
  235.8 2.3 copy.18
  238.1 0.0 copy-done
  238.1 0.7 copy.19
Async XLA Ops:
  235.8 2.3 copy-start
